TPU v7x, 256 devices: a whole 4x4x8 slice. The times are simulated.
256 devices in a mesh: aa: 16 (over x, z_lo), ba: 16 (over z_hi, y, core).
Axes of the slice: x: 4, y: 4, z: 8 (z_hi: 2, z_lo: 4; z = z_hi * 4 + z_lo), core: 2. Of those that a mesh axis runs over, the one named last changes fastest.
Arguments:
- tokens: bfloat16 [16, 64, 256, 256], P('aa', 'ba'), may hold values from -6 to 6
- gain_attn: float32 [256], replicated, may hold values from 0.5 to 1.5
- fine_qkv: bfloat16 [256, 768], replicated, may hold values from -0.375 to 0.375
- fine_scale: float32 [4], replicated, may hold values from 8 to 32
- fine_out: bfloat16 [256, 256], replicated, may hold values from -0.375 to 0.375
- gain_mlp: float32 [256], replicated, may hold values from 0.5 to 1.5
- mlp_in: bfloat16 [256, 1536], replicated, may hold values from -0.375 to 0.375
- mlp_out: bfloat16 [768, 256], replicated, may hold values from -0.21875 to 0.21875
- merge_one: bfloat16 [1024, 512], P('aa'), may hold values from -0.1875 to 0.1875
- merge_two: bfloat16 [2048, 1024], P('aa'), may hold values from -0.125 to 0.125
- coarse_gain: float32 [1024], replicated, may hold values from 0.5 to 1.5
- coarse_qkv: bfloat16 [1024, 3072], P('aa'), may hold values from -0.1875 to 0.1875
- time_scale: float32 [16], replicated, may hold values from 8 to 32
- space_scale: float32 [16], replicated, may hold values from 8 to 32
- coarse_out: bfloat16 [2048, 1024], P('aa'), may hold values from -0.375 to 0.375
- split_two: bfloat16 [1024, 2048], P('aa'), may hold values from -0.1875 to 0.1875
- lerp_two: float32 [512], replicated, may hold values from 0.25 to 0.75
- split_one: bfloat16 [512, 1024], P('aa'), may hold values from -0.25 to 0.25
- lerp_one: float32 [256], replicated, may hold values from 0.25 to 0.75
Outputs:
- refined: bfloat16 [16, 64, 256, 256], P('aa', 'ba')
All inputs are finite; a program needn't handle non-finite values.
Results may differ from a plain program's by a relative error of at most 0.014.
Values may be sent and summed in bfloat16 or wider, within the bound.
No kernel may reach another device: no remote copies, remote signals or barrier semaphores. Data moves between devices by JAX's collectives and lax.ppermute only.
A program may use at most 128 MiB of HBM per device.

v0:
```python
import math

import jax
import jax.numpy as jnp
from jax import lax
from jax.sharding import Mesh
from jax.sharding import PartitionSpec as P

AA = ("aa_0", "aa_1")


EPS = 1e-06


def with_halo(cells, sides, width):
    for axis, dim in sides:
        count = lax.axis_size(axis)
        ends = count - 1
        head = lax.slice_in_dim(cells, 0, width, axis=dim)
        tail = lax.slice_in_dim(cells, cells.shape[dim] - width, cells.shape[dim], axis=dim)
        cells = jnp.concatenate(
            [
                lax.ppermute(tail, axis, [(i, (i + 1) % count) for i in range(ends)]),
                cells,
                lax.ppermute(head, axis, [((i + 1) % count, i) for i in range(ends)]),
            ],
            axis=dim,
        )
    return cells


def sent_to_all(shard, axis):
    length = lax.axis_size(axis)
    return lax.all_to_all(
        jnp.broadcast_to(shard[None], (length, *shard.shape)), axis, 0, 0, tiled=True
    )


def in_order(tiles, dim):
    lengths = list(tiles.shape[1:])
    lengths[dim] *= tiles.shape[0]
    return jnp.moveaxis(tiles, 0, dim).reshape(lengths)


def collect(shard, axis, dim):
    tiles = sent_to_all(shard, axis)
    return in_order(tiles, dim)


def whole_of(shard, axes, dim):
    if not axes:
        return shard
    nearer = lax.all_gather(shard, axes[-1], axis=dim, tiled=True)
    return whole_of(nearer, axes[:-1], dim)


def rms_scale(value, gain):
    return value * lax.rsqrt(jnp.mean(value * value, axis=-1, keepdims=True) + EPS) * gain


def unit_axis(value, axis):
    return value * lax.rsqrt(jnp.mean(value * value, axis=axis, keepdims=True) + EPS)


def to_grid(part, head_size):
    row_count, col_count, width = part.shape
    return part.reshape(row_count, col_count, width // head_size, head_size).transpose(2, 3, 0, 1)


def window_attention(queries, key_grid, value_grid, row_ok, col_ok, scales):
    head_count, head_size, row_count, col_count = queries.shape
    factor = (scales / head_size)[:, None, None]
    query_wide = queries.astype(jnp.float32)
    weights = []
    for shift_row in range(7):
        for shift_col in range(7):
            key_part = key_grid[
                :, :, shift_row : shift_row + row_count, shift_col : shift_col + col_count
            ].astype(jnp.float32)
            scores = jnp.sum(query_wide * key_part, axis=1) * factor
            usable = (
                row_ok[shift_row : shift_row + row_count, None]
                * col_ok[None, shift_col : shift_col + col_count]
            )
            weights.append(jnp.exp(scores) * usable)
    weight_sum = jnp.sum(jnp.stack(weights), axis=0)
    numerator = jnp.zeros(queries.shape, jnp.float32)
    for shift_row in range(7):
        for shift_col in range(7):
            value_part = value_grid[
                :, :, shift_row : shift_row + row_count, shift_col : shift_col + col_count
            ].astype(jnp.float32)
            numerator = numerator + weights[shift_row * 7 + shift_col][:, None] * value_part
    return numerator / weight_sum[:, None]


def finish_fine(stream, attended, fine_out, gain_mlp, mlp_in, mlp_out):
    row_count, col_count, width = stream.shape
    attended = (
        attended.transpose(2, 3, 0, 1).reshape(row_count * col_count, width).astype(jnp.bfloat16)
    )
    stream = stream + jnp.dot(attended, fine_out, preferred_element_type=jnp.float32).reshape(
        row_count, col_count, width
    )
    normed = rms_scale(stream, gain_mlp).astype(jnp.bfloat16)
    lifted = jnp.dot(normed.reshape(-1, width), mlp_in, preferred_element_type=jnp.float32)
    hidden_count = mlp_out.shape[0]
    hidden = (jax.nn.gelu(lifted[:, :hidden_count]) * lifted[:, hidden_count:]).astype(jnp.bfloat16)
    stream = stream + jnp.dot(hidden, mlp_out, preferred_element_type=jnp.float32).reshape(
        row_count, col_count, width
    )
    return stream.astype(jnp.bfloat16)


def patch_merge(grid):
    frame_count, row_count, col_count, width = grid.shape
    moved = grid.reshape(frame_count, row_count // 2, 2, col_count // 2, 2, width).transpose(
        0, 1, 3, 2, 4, 5
    )
    return moved.reshape(frame_count, row_count // 2, col_count // 2, 4 * width)


def patch_split(flat, frame_count, row_count, col_count):
    width = flat.shape[1] // 4
    moved = flat.reshape(frame_count, row_count, col_count, 2, 2, width).transpose(0, 1, 3, 2, 4, 5)
    return moved.reshape(frame_count, 2 * row_count, 2 * col_count, width)


def temporal(packed, scales):
    frame_count, place_count, total_width = packed.shape
    head_count = scales.shape[0]
    head_size = total_width // (3 * head_count)
    split_parts = packed.reshape(frame_count, place_count, head_count, 3, head_size)
    queries = lax.optimization_barrier(
        unit_axis(split_parts[:, :, :, 0].astype(jnp.float32), 3).astype(jnp.bfloat16)
    )
    key_part = lax.optimization_barrier(
        unit_axis(split_parts[:, :, :, 1].astype(jnp.float32), 3).astype(jnp.bfloat16)
    )
    value_part = split_parts[:, :, :, 2]
    scores = jnp.einsum("fphd,gphd->phfg", queries, key_part, preferred_element_type=jnp.float32)
    weights = jnp.exp(scores * (scales / head_size)[None, :, None, None])
    weight_sum = jnp.sum(weights, axis=3)
    rounded = lax.optimization_barrier(weights.astype(jnp.bfloat16))
    merged = jnp.einsum("phfg,gphd->fphd", rounded, value_part, preferred_element_type=jnp.float32)
    merged = merged / weight_sum.transpose(2, 0, 1)[:, :, :, None]
    return merged.reshape(frame_count, place_count, head_count * head_size).astype(jnp.bfloat16)


def spatial(packed, scales):
    place_count, total_width = packed.shape
    head_count = scales.shape[0]
    head_size = total_width // (3 * head_count)
    split_parts = packed.reshape(place_count, head_count, 3, head_size)
    queries = (
        unit_axis(split_parts[:, :, 0].astype(jnp.float32), 2)
        .astype(jnp.bfloat16)
        .transpose(1, 0, 2)
    )
    key_part = (
        unit_axis(split_parts[:, :, 1].astype(jnp.float32), 2)
        .astype(jnp.bfloat16)
        .transpose(1, 0, 2)
    )
    value_part = split_parts[:, :, 2].transpose(1, 0, 2)
    block_rows = math.gcd(place_count, 512)
    factor = (scales / head_size)[:, None, None]
    blocks = queries.reshape(
        head_count, place_count // block_rows, block_rows, head_size
    ).transpose(1, 0, 2, 3)

    def one_block(query_block):
        scores = (
            jnp.einsum("hqd,hkd->hqk", query_block, key_part, preferred_element_type=jnp.float32)
            * factor
        )
        weights = jnp.exp(scores)
        weight_sum = jnp.sum(weights, axis=2)
        merged = jnp.einsum(
            "hqk,hkd->hqd",
            weights.astype(jnp.bfloat16),
            value_part,
            preferred_element_type=jnp.float32,
        )
        return merged / weight_sum[:, :, None]

    results = lax.map(one_block, blocks)
    return (
        results.transpose(0, 2, 1, 3)
        .reshape(place_count, head_count * head_size)
        .astype(jnp.bfloat16)
    )


def row_product(operand, weight_rows):
    return jnp.dot(operand, weight_rows, preferred_element_type=jnp.float32)


def shards(
    tokens,
    gain_attn,
    fine_qkv,
    fine_scale,
    fine_out,
    gain_mlp,
    mlp_in,
    mlp_out,
    merge_one,
    merge_two,
    coarse_gain,
    coarse_qkv,
    time_scale,
    space_scale,
    coarse_out,
    split_two,
    lerp_two,
    split_one,
    lerp_one,
):
    frame_count, row_count, col_count, width = tokens.shape
    head_size = width // fine_scale.shape[0]
    stream = tokens.astype(jnp.float32)
    normed = rms_scale(stream, gain_attn).astype(jnp.bfloat16)
    packed = jnp.dot(
        normed.reshape(-1, width), fine_qkv, preferred_element_type=jnp.float32
    ).astype(jnp.bfloat16)
    packed = packed.reshape(frame_count, row_count, col_count, 3 * width)
    border = with_halo(tokens, (("ba", 1),), 3)
    outer_rows = jnp.concatenate([border[:, :3], border[:, row_count + 3 :]], axis=1)
    outer_normed = rms_scale(outer_rows.astype(jnp.float32), gain_attn).astype(jnp.bfloat16)
    outer_packed = jnp.dot(
        outer_normed.reshape(-1, width), fine_qkv[:, width:], preferred_element_type=jnp.float32
    ).astype(jnp.bfloat16)
    outer_packed = outer_packed.reshape(frame_count, 6, col_count, 2 * width)
    key_value = jnp.concatenate(
        [outer_packed[:, :3], packed[:, :, :, width:], outer_packed[:, 3:]], axis=1
    )
    first_row = lax.axis_index("ba") * row_count - 3
    global_rows = first_row + jnp.arange(row_count + 6, dtype=jnp.int32)
    row_ok = ((global_rows >= 0) & (global_rows < row_count * lax.axis_size("ba"))).astype(
        jnp.float32
    )
    col_ok = jnp.pad(jnp.ones((col_count,), jnp.float32), 3)

    def fine_one(frame_parts):
        frame_stream, frame_packed, frame_near = frame_parts
        queries = lax.optimization_barrier(
            unit_axis(to_grid(frame_packed[:, :, :width], head_size).astype(jnp.float32), 1).astype(
                jnp.bfloat16
            )
        )
        key_grid = lax.optimization_barrier(
            unit_axis(to_grid(frame_near[:, :, :width], head_size).astype(jnp.float32), 1).astype(
                jnp.bfloat16
            )
        )
        value_grid = to_grid(frame_near[:, :, width:], head_size)
        margin = ((0, 0), (0, 0), (0, 0), (3, 3))
        key_grid = jnp.pad(key_grid, margin)
        value_grid = jnp.pad(value_grid, margin)
        attended = window_attention(queries, key_grid, value_grid, row_ok, col_ok, fine_scale)
        return finish_fine(frame_stream, attended, fine_out, gain_mlp, mlp_in, mlp_out)

    level_zero = lax.map(fine_one, (stream, packed, key_value))
    flat_one = patch_merge(level_zero).reshape(-1, 4 * width)
    level_one = row_product(flat_one, collect(merge_one, AA, 0)).astype(jnp.bfloat16)
    grid_one = level_one.reshape(frame_count, row_count // 2, col_count // 2, -1)
    flat_two = patch_merge(grid_one).reshape(-1, 4 * grid_one.shape[3])
    coarse = row_product(flat_two, lax.all_gather(merge_two, AA, axis=0, tiled=True))
    coarse_width = coarse.shape[1]
    place_count = row_count // 4 * (col_count // 4)
    slab_count = lax.axis_size(AA)
    per_slab = place_count // slab_count
    normed = rms_scale(coarse, coarse_gain).astype(jnp.bfloat16)
    whole_qkv = lax.all_gather(coarse_qkv, AA, axis=0, tiled=True)
    packed = jnp.dot(normed, whole_qkv, preferred_element_type=jnp.float32).astype(jnp.bfloat16)
    grouped = normed.reshape(frame_count, slab_count, per_slab, coarse_width)
    moved = lax.all_to_all(grouped, AA, split_axis=1, concat_axis=0, tiled=True)
    projected = jnp.dot(
        moved.reshape(-1, coarse_width), whole_qkv, preferred_element_type=jnp.float32
    ).astype(jnp.bfloat16)
    projected = projected.reshape(moved.shape[0], moved.shape[2], 3 * coarse_width)
    time_out = temporal(projected, time_scale).reshape(
        moved.shape[0], 1, moved.shape[2], coarse_width
    )
    time_out = lax.all_to_all(time_out, AA, split_axis=0, concat_axis=1, tiled=True).reshape(
        frame_count * place_count, coarse_width
    )
    head_groups = lax.axis_size("ba")
    local_heads = time_scale.shape[0] // head_groups
    local_scale = lax.dynamic_slice_in_dim(
        space_scale, lax.axis_index("ba") * local_heads, local_heads
    )
    group_width = 3 * coarse_width // head_groups
    grouped = packed.reshape(frame_count, place_count, head_groups, group_width)
    space_out = lax.map(
        lambda single_frame: spatial(single_frame[:, 0], local_scale),
        lax.all_to_all(grouped, "ba", split_axis=2, concat_axis=1, tiled=True),
    )[:, :, None]
    space_out = lax.all_to_all(space_out, "ba", split_axis=1, concat_axis=2, tiled=True).reshape(
        frame_count * place_count, coarse_width
    )
    attended = jnp.concatenate([time_out, space_out], axis=1)
    coarse = coarse + row_product(attended, lax.all_gather(coarse_out, AA, axis=0, tiled=True))
    coarse_narrow = coarse.astype(jnp.bfloat16)
    raised = row_product(coarse_narrow, whole_of(split_two, AA, 0))
    raised_grid = patch_split(raised, frame_count, row_count // 4, col_count // 4)
    skip_one = grid_one.astype(jnp.float32)
    blended = (skip_one + lerp_two * (raised_grid - skip_one)).astype(jnp.bfloat16)
    flat_blend = blended.reshape(-1, blended.shape[3])
    raised = row_product(flat_blend, collect(split_one, AA, 0))
    raised_grid = patch_split(raised, frame_count, row_count // 2, col_count // 2)
    skip_zero = level_zero.astype(jnp.float32)
    return (skip_zero + lerp_one * (raised_grid - skip_zero)).astype(jnp.bfloat16)


def solution(mesh):
    torus = Mesh(mesh.devices.reshape(4, 4, mesh.shape["ba"]), ("aa_0", "aa_1", "ba"))
    return jax.shard_map(
        shards,
        mesh=torus,
        in_specs=(
            P(AA, "ba", None, None),
            P(),
            P(),
            P(),
            P(),
            P(),
            P(),
            P(),
            P(AA, None),
            P(AA, None),
            P(),
            P(AA, None),
            P(),
            P(),
            P(AA, None),
            P(AA, None),
            P(),
            P(AA, None),
            P(),
        ),
        out_specs=P(AA, "ba", None, None),
        check_vma=False,
    )
```

profile of v0, /device:TPU:1, one launch (start us, length us, event | category | flops | bytes accessed | tf_op | source)
XLA Modules:
  0.0 507.3 jit_solution(16369285541483502025)
XLA Ops:
  8.8 37.0 %all-gather.12.cloned.1.call-done = bf16[256,2048]{1,0:T(8,128)(2,1)} async-done(((bf16[64,2048]{1,0:T(8,128)(2,1)}), bf16[256,2048]{1,0:T(8,128)(2,1)}) %all-gather.12.cloned.1.call-update) | async-done | bytes 1048592 | tf_op jit(solution)/shard_map/all_gather | solution.py:53
  46.7 4.5 collective-permute-start
  54.2 4.6 all-to-all-start
  78.8 4.3 fusion.39
  83.1 4.1 fusion.40
  92.4 10.3 %divide_convert_fusion = bf16[4,64,4,256]{3,1,0,2:T(8,128)(2,1)S(1)} fusion(bf16[4,64,10,256]{3,1,0,2:T(8,128)(2,1)S(1)} %bitcast.179, f32[4,4,256]{2,0,1:T(4,128)S(1)} %get-tuple-element.167, f32[4,4,256]{2,0,1:T(4,128)S(1)} %get-tuple-element.216, f32[4,4,256]{2,0,1:T(4,128)S(1)} %get-tuple-element.215, f32[4,4,256]{2,0,1:T(4,128)S(1)} %get-tuple-element.214, ...), kind=kLoop, calls=%fused_computation.249 | loop fusion | flops 38797312 | bytes 6324224 | tf_op jit(solution)/shard_map/while/body/eval_jaxpr/convert_element_type | solution.py:100
  107.2 8.0 %all-to-all-done = bf16[16,64,512]{2,1,0:T(8,128)(2,1)} async-done(((bf16[16,64,512]{2,1,0:T(8,128)(2,1)}), bf16[16,64,512]{2,1,0:T(8,128)(2,1)}, u32[]{:S(2)}, u32[]{:S(2)}) %all-to-all-start) | async-done | bytes 1048608 | tf_op jit(solution)/shard_map/all_to_all | solution.py:34
  117.4 54.4 %all-gather.6.cloned.1.call-done = bf16[2048,1024]{1,0:T(8,128)(2,1)} async-done(((bf16[128,1024]{1,0:T(8,128)(2,1)}), bf16[2048,1024]{1,0:T(8,128)(2,1)}) %all-gather.6.cloned.1.call-update) | async-done | bytes 4194320 | tf_op jit(solution)/shard_map/all_gather | solution.py:269
  171.8 3.1 multiply_reduce_fusion.5
  175.8 5.0 all-to-all-start.1
  182.2 5.9 %all-to-all-done.1 = bf16[1,16,4,1024]{3,2,0,1:T(4,128)(2,1)S(1)} async-done(((bf16[1,16,4,1024]{3,2,0,1:T(4,128)(2,1)}), bf16[1,16,4,1024]{3,2,0,1:T(4,128)(2,1)S(1)}, u32[]{:S(2)}, u32[]{:S(2)}) %all-to-all-start.1) | async-done | bytes 131104 | tf_op jit(solution)/shard_map/all_to_all | solution.py:278
  188.1 128.7 %all-gather.8.cloned.1.call-done = bf16[1024,3072]{1,0:T(8,128)(2,1)} async-done(((bf16[64,3072]{1,0:T(8,128)(2,1)}), bf16[1024,3072]{1,0:T(8,128)(2,1)}) %all-gather.8.cloned.1.call-update) | async-done | bytes 6291472 | tf_op jit(solution)/shard_map/all_gather | solution.py:275
  316.8 4.0 convolution_convert_fusion.1
  321.7 4.0 convolution_convert_fusion
  327.3 7.8 %all-to-all-start.3 = ((bf16[1,64,16,192]{3,1,0,2:T(8,128)(2,1)}), bf16[1,64,16,192]{3,1,0,2:T(8,128)(2,1)}, u32[]{:S(2)}, u32[]{:S(2)}) async-start(bf16[1,64,16,192]{3,1,0,2:T(8,128)(2,1)} %copy.84), calls=%async_computation.3 | async-start | bytes 1048576 | tf_op jit(solution)/shard_map/all_to_all | solution.py:298
  337.9 13.2 %all-to-all-done.3 = bf16[1,64,16,192]{3,1,0,2:T(8,128)(2,1)} async-done(((bf16[1,64,16,192]{3,1,0,2:T(8,128)(2,1)}), bf16[1,64,16,192]{3,1,0,2:T(8,128)(2,1)}, u32[]{:S(2)}, u32[]{:S(2)}) %all-to-all-start.3) | async-done | bytes 393248 | tf_op jit(solution)/shard_map/all_to_all | solution.py:298
  352.2 6.0 %all-to-all-start.5 = ((bf16[16,32,1024]{2,1,0:T(8,128)(2,1)}), bf16[16,32,1024]{2,1,0:T(8,128)(2,1)S(1)}, u32[]{:S(2)}, u32[]{:S(2)}) async-start(bf16[16,32,1024]{2,1,0:T(8,128)(2,1)} %broadcast_in_dim.139), calls=%async_computation.5 | async-start | bytes 2097152 | tf_op jit(solution)/shard_map/all_to_all | solution.py:34
  366.3 18.9 %all-to-all-done.5 = bf16[16,32,1024]{2,1,0:T(8,128)(2,1)S(1)} async-done(((bf16[16,32,1024]{2,1,0:T(8,128)(2,1)}), bf16[16,32,1024]{2,1,0:T(8,128)(2,1)S(1)}, u32[]{:S(2)}, u32[]{:S(2)}) %all-to-all-start.5) | async-done | bytes 1048608 | tf_op jit(solution)/shard_map/all_to_all | solution.py:34
  385.2 4.3 all-to-all-start.2
  395.6 3.1 all-to-all-done.2
  398.7 7.4 %all-to-all-start.4 = ((bf16[16,2,2048]{2,1,0:T(2,128)(2,1)}), bf16[16,2,2048]{2,1,0:T(2,128)(2,1)S(1)}, u32[]{:S(2)}, u32[]{:S(2)}) async-start(bf16[16,2,2048]{2,1,0:T(2,128)(2,1)} %reshape.2296), calls=%async_computation.4 | async-start | bytes 262144 | tf_op jit(solution)/shard_map/all_to_all | solution.py:300
  407.4 10.5 %all-to-all-done.4 = bf16[16,2,2048]{2,1,0:T(2,128)(2,1)S(1)} async-done(((bf16[16,2,2048]{2,1,0:T(2,128)(2,1)}), bf16[16,2,2048]{2,1,0:T(2,128)(2,1)S(1)}, u32[]{:S(2)}, u32[]{:S(2)}) %all-to-all-start.4) | async-done | bytes 131104 | tf_op jit(solution)/shard_map/all_to_all | solution.py:300
  419.4 66.0 %all-gather.10.cloned.1.call-done = bf16[2048,1024]{1,0:T(8,128)(2,1)} async-done(((bf16[128,1024]{1,0:T(8,128)(2,1)}), bf16[2048,1024]{1,0:T(8,128)(2,1)}) %all-gather.10.cloned.1.call-update) | async-done | bytes 4194320 | tf_op jit(solution)/shard_map/all_gather | solution.py:304
  485.5 5.0 fusion.33
  (252 shorter events, 73.3 us)
Async XLA Ops:
  6.5 97.0 %copy-start = (bf16[256,1536]{1,0:T(8,128)(2,1)S(1)}, bf16[256,1536]{1,0:T(8,128)(2,1)}, u32[]{:S(2)}) copy-start(bf16[256,1536]{1,0:T(8,128)(2,1)} %param.27) | copy-start | bytes 2359300
  6.5 39.2 %copy-start.2 = (bf16[1,4,256,256]{3,2,1,0:T(8,128)(2,1)S(1)}, bf16[1,4,256,256]{3,2,1,0:T(8,128)(2,1)}, u32[]{:S(2)}) copy-start(bf16[1,4,256,256]{3,2,1,0:T(8,128)(2,1)} %param.21) | copy-start | bytes 1572868
  6.5 46.6 %copy-start.9 = (bf16[64,512]{1,0:T(8,128)(2,1)S(1)}, bf16[64,512]{1,0:T(8,128)(2,1)}, u32[]{:S(2)}) copy-start(bf16[64,512]{1,0:T(8,128)(2,1)} %param.29) | copy-start | bytes 196612
  6.5 39.2 %all-gather.12.cloned.1.call-start = ((), (), s32[]{:S(2)}) async-start(), calls=%async_computation.9 | async-start | bytes 1310720 | tf_op jit(solution)/shard_map/all_gather | solution.py:53
  7.3 164.5 %all-gather.6.cloned.1.call-start = ((), (), s32[]{:S(2)}) async-start(), calls=%async_computation.6 | async-start | bytes 4456448 | tf_op jit(solution)/shard_map/all_gather | solution.py:269
  8.0 308.8 %all-gather.8.cloned.1.call-start = ((), (), s32[]{:S(2)}) async-start(), calls=%async_computation.7 | async-start | bytes 6684672 | tf_op jit(solution)/shard_map/all_gather | solution.py:275
  8.7 410.7 %all-gather.14.cloned.1.call-start = ((), (), s32[]{:S(2)}) async-start(), calls=%async_computation.10 | async-start | bytes 5242880 | tf_op jit(solution)/shard_map/all_gather | solution.py:53
  46.7 20.2 %collective-permute-start = (bf16[1,3,256,256]{3,2,1,0:T(8,128)(2,1)}, bf16[1,3,256,256]{3,2,1,0:T(8,128)(2,1)S(1)}, u32[]{:S(2)}, u32[]{:S(2)}) collective-permute-start(bf16[1,3,256,256]{3,2,1,0:T(8,128)(2,1)} %get-tuple-element.228), channel_id=1, source_target_pairs={{0,1},{1,2},{2,3},{3,4},{4,5},{5,6},{6,7},{7,8},{8,9},{9,10},{10,1... | collective-permute-start | bytes 1179656 | tf_op jit(solution)/shard_map/ppermute | solution.py:23
  51.2 8.5 %copy-start.58 = (f32[256]{0:T(256)S(1)}, f32[256]{0:T(256)}, u32[]{:S(2)}) copy-start(f32[256]{0:T(256)} %param.22) | copy-start | bytes 3076
  51.2 15.8 %collective-permute-start.1 = (bf16[1,3,256,256]{3,2,1,0:T(8,128)(2,1)}, bf16[1,3,256,256]{3,2,1,0:T(8,128)(2,1)}, u32[]{:S(2)}, u32[]{:S(2)}) collective-permute-start(bf16[1,3,256,256]{3,2,1,0:T(8,128)(2,1)} %get-tuple-element.229), channel_id=1, source_target_pairs={{1,0},{2,1},{3,2},{4,3},{5,4},{6,5},{7,6},{8,7},{9,8},{10,9},{11,1... | collective-permute-start | bytes 1179656 | tf_op jit(solution)/shard_map/ppermute | solution.py:25
  54.2 5.7 %copy-start.6 = (bf16[256,768]{1,0:T(8,128)(2,1)S(1)}, bf16[256,768]{1,0:T(8,128)(2,1)}, u32[]{:S(2)}) copy-start(bf16[256,768]{1,0:T(8,128)(2,1)} %param.23) | copy-start | bytes 1179652
  54.2 61.0 %all-to-all-start = ((bf16[16,64,512]{2,1,0:T(8,128)(2,1)}), bf16[16,64,512]{2,1,0:T(8,128)(2,1)}, u32[]{:S(2)}, u32[]{:S(2)}) async-start(bf16[16,64,512]{2,1,0:T(8,128)(2,1)} %broadcast_in_dim.137), calls=%async_computation | async-start | bytes 2097152 | tf_op jit(solution)/shard_map/all_to_all | solution.py:34
  58.8 426.6 %all-gather.10.cloned.1.call-start = ((), (), s32[]{:S(2)}) async-start(), calls=%async_computation.8 | async-start | bytes 4456448 | tf_op jit(solution)/shard_map/all_gather | solution.py:304
  92.3 10.3 %copy-start.8 = (bf16[256,256]{1,0:T(8,128)(2,1)S(1)}, bf16[256,256]{1,0:T(8,128)(2,1)}, u32[]{:S(2)}) copy-start(bf16[256,256]{1,0:T(8,128)(2,1)} %param.25) | copy-start | bytes 393220
  117.4 57.6 %copy-start.57 = (f32[1024]{0:T(1024)S(1)}, f32[1024]{0:T(1024)}, u32[]{:S(2)}) copy-start(f32[1024]{0:T(1024)} %param.31) | copy-start | bytes 12292
  117.4 63.4 %copy-start.64 = (f32[16]{0:T(128)S(1)}, f32[16]{0:T(128)}, u32[]{:S(2)}) copy-start(f32[16]{0:T(128)} %param.34) | copy-start | bytes 196
  117.4 64.8 %copy-start.65 = (f32[16]{0:T(128)S(1)}, f32[16]{0:T(128)}, u32[]{:S(2)}) copy-start(f32[16]{0:T(128)} %param.33) | copy-start | bytes 196
  175.8 12.3 %all-to-all-start.1 = ((bf16[1,16,4,1024]{3,2,0,1:T(4,128)(2,1)}), bf16[1,16,4,1024]{3,2,0,1:T(4,128)(2,1)S(1)}, u32[]{:S(2)}, u32[]{:S(2)}) async-start(bf16[1,16,4,1024]{3,2,0,1:T(4,128)(2,1)} %bitcast.29), calls=%async_computation.1 | async-start | bytes 262144 | tf_op jit(solution)/shard_map/all_to_all | solution.py:278
  327.3 23.8 %all-to-all-start.3 = ((bf16[1,64,16,192]{3,1,0,2:T(8,128)(2,1)}), bf16[1,64,16,192]{3,1,0,2:T(8,128)(2,1)}, u32[]{:S(2)}, u32[]{:S(2)}) async-start(bf16[1,64,16,192]{3,1,0,2:T(8,128)(2,1)} %copy.84), calls=%async_computation.3 | async-start | bytes 1048576 | tf_op jit(solution)/shard_map/all_to_all | solution.py:298
  335.1 16.0 %copy-start.10 = (bf16[32,1024]{1,0:T(8,128)(2,1)S(1)}, bf16[32,1024]{1,0:T(8,128)(2,1)}, u32[]{:S(2)}) copy-start(bf16[32,1024]{1,0:T(8,128)(2,1)} %param.38) | copy-start | bytes 196612
  352.2 33.0 %all-to-all-start.5 = ((bf16[16,32,1024]{2,1,0:T(8,128)(2,1)}), bf16[16,32,1024]{2,1,0:T(8,128)(2,1)S(1)}, u32[]{:S(2)}, u32[]{:S(2)}) async-start(bf16[16,32,1024]{2,1,0:T(8,128)(2,1)} %broadcast_in_dim.139), calls=%async_computation.5 | async-start | bytes 2097152 | tf_op jit(solution)/shard_map/all_to_all | solution.py:34
  385.2 13.5 %all-to-all-start.2 = ((bf16[16,1,4,1024]{3,2,1,0:T(4,128)(2,1)}), bf16[16,1,4,1024]{3,2,1,0:T(4,128)(2,1)S(1)}, u32[]{:S(2)}, u32[]{:S(2)}) async-start(bf16[16,1,4,1024]{3,2,1,0:T(4,128)(2,1)} %reshape.2294), calls=%async_computation.2 | async-start | bytes 262144 | tf_op jit(solution)/shard_map/all_to_all | solution.py:286
  398.7 19.3 %all-to-all-start.4 = ((bf16[16,2,2048]{2,1,0:T(2,128)(2,1)}), bf16[16,2,2048]{2,1,0:T(2,128)(2,1)S(1)}, u32[]{:S(2)}, u32[]{:S(2)}) async-start(bf16[16,2,2048]{2,1,0:T(2,128)(2,1)} %reshape.2296), calls=%async_computation.4 | async-start | bytes 262144 | tf_op jit(solution)/shard_map/all_to_all | solution.py:300
  495.6 4.7 copy-start.1
  (55 other events, 167.6 us)
Sparse Core Ops, SparseCore 0:
  9.1 36.5 all-gather.11
  47.5 124.2 all-gather.5
  173.6 143.1 all-gather.7
  318.5 57.1 all-gather.13
  377.3 108.1 all-gather.9
where the time goes:
time: 518 us; the launch traced here: 507 us
  waiting for transfers between devices  348 us (67%)
  starting transfers between devices  41.7 us (8%)
  other arithmetic  39.7 us (8%)
  local copies, waits for them, and re-layouts  35.5 us (7%)
  matrix products  26.2 us (5%)
  between operations  15.8 us (3%)
    all_gather x1, waiting for transfers between devices, shards(): whole_qkv = lax.all_gather(coarse_qkv, AA, axis=0, tiled=True)  129 us
    all_gather x1, waiting for transfers between devices, shards(): lax.all_gather(coarse_out, AA, axis=0, tiled=True)  66 us
    all_gather x1, waiting for transfers between devices, shards(): lax.all_gather(merge_two, AA, axis=0, tiled=True)  54.4 us
    all_gather x2, waiting for transfers between devices, whole_of(): nearer = lax.all_gather(shard, axes[-1], axis=dim, tiled=True)  37 us
    all_to_all x2, waiting for transfers between devices, sent_to_all(): lax.all_to_all(jnp.broadcast_to(shard[None], (length, *shard.shape)), axi...  27 us
    all_to_all x1, waiting for transfers between devices, shards(): lax.all_to_all(grouped, 'ba', split_axis=2, concat_axis=1, tiled=True)  13.2 us
    reduce_sum x3, other arithmetic, window_attention(): scores = jnp.sum(query_wide * key_part, axis=1) * factor  11.2 us
    all_to_all x2, starting transfers between devices, sent_to_all(): lax.all_to_all(jnp.broadcast_to(shard[None], (length, *shard.shape)), axi...  10.6 us
  transfers between devices with their start and end apart: 13, of which 10 were waited for; matrix products, arithmetic and copies ran while one was open for 17% of the time, Pallas kernels for 0%

commit v1 on v0

v1 whole, which is shorter than its diff:
```python
import jax
import jax.numpy as jnp
from jax import lax
from jax.experimental import pallas as pl
from jax.experimental.pallas import tpu as pltpu
from jax.sharding import Mesh
from jax.sharding import PartitionSpec as P

AA = ("x", "zl")
BA = ("zh", "yh", "yl", "c")
GROUP = ("yl", "c")
ACROSS = ("zh", "yh")
Y = ("yh", "yl")

EPS = 1e-06
HALO = 3
PAD = 16
TILE = 64
SPAN = TILE + 2 * PAD
HEAD = 64
FAR = -1e30
F32 = jnp.float32
BF16 = jnp.bfloat16
VMEM_LIMIT = 60 * 1024 * 1024


def dot(a, b):
    return jnp.dot(a, b, preferred_element_type=F32)


def dot_nt(a, b):
    return lax.dot_general(a, b, (((1,), (1,)), ((), ())), preferred_element_type=F32)


def rms_scale(value, gain):
    return value * lax.rsqrt(jnp.mean(value * value, axis=-1, keepdims=True) + EPS) * gain


def head_sums(width):
    row = lax.broadcasted_iota(jnp.int32, (width, width), 0) // HEAD
    col = lax.broadcasted_iota(jnp.int32, (width, width), 1) // HEAD
    return jnp.where(row == col, 1.0 / HEAD, 0.0).astype(BF16)


def unit_heads(value, sums):
    square = value * value
    high = square.astype(BF16)
    low = (square - high.astype(F32)).astype(BF16)
    return value * lax.rsqrt(dot(high, sums) + dot(low, sums) + EPS)


def call(body, out_shape, scratch=(), smem=0, count=0):
    specs = [pl.BlockSpec(memory_space=pltpu.SMEM)] * smem + [
        pl.BlockSpec(memory_space=pltpu.VMEM)
    ] * (count - smem)
    return pl.pallas_call(
        body,
        in_specs=specs,
        out_shape=out_shape,
        scratch_shapes=list(scratch),
        compiler_params=pltpu.CompilerParams(vmem_limit_bytes=VMEM_LIMIT),
    )


def fine_body(
    place_ref,
    scale_ref,
    own_ref,
    above_ref,
    below_ref,
    gain_ref,
    qkv_ref,
    out_w_ref,
    gain_mlp_ref,
    mlp_in_ref,
    mlp_out_ref,
    level_ref,
    flat_ref,
    q_s,
    k_s,
    v_s,
    mix_s,
    row_s,
):
    rows, cols, width = own_ref.shape
    heads = width // HEAD
    sums = head_sums(width)
    gain = gain_ref[...]
    edge = jnp.zeros((PAD, width), BF16)
    for r in range(rows + 2 * HALO):
        own = HALO <= r < HALO + rows
        if own:
            tile = own_ref[r - HALO]
        elif r < HALO:
            tile = above_ref[r]
        else:
            tile = below_ref[r - HALO - rows]
        normed = rms_scale(tile.astype(F32), gain).astype(BF16)
        if own:
            q = dot(normed, qkv_ref[:, :width]).astype(BF16)
            q_s[r - HALO] = unit_heads(q.astype(F32), sums).astype(BF16)
        k = dot(normed, qkv_ref[:, width : 2 * width]).astype(BF16)
        v = dot(normed, qkv_ref[:, 2 * width :]).astype(BF16)
        k_s[r, pl.ds(PAD, cols), :] = unit_heads(k.astype(F32), sums).astype(BF16)
        v_s[r, pl.ds(PAD, cols), :] = v
        k_s[r, pl.ds(0, PAD), :] = edge
        v_s[r, pl.ds(0, PAD), :] = edge
        k_s[r, pl.ds(PAD + cols, PAD), :] = edge
        v_s[r, pl.ds(PAD + cols, PAD), :] = edge

    reach = 2 * HALO + 1
    keys = reach * SPAN
    key_lane = lax.broadcasted_iota(jnp.int32, (TILE, keys), 1)
    shift = key_lane % SPAN - PAD - lax.broadcasted_iota(jnp.int32, (TILE, keys), 0)
    band = (shift >= -HALO) & (shift <= HALO)
    key_col = key_lane % SPAN - PAD
    key_row = key_lane // SPAN - HALO
    lane_head = lax.broadcasted_iota(jnp.int32, (TILE, width), 1) // HEAD
    total_rows = place_ref[1]
    tiles = cols // TILE

    def one_tile(step, carry):
        r = step // tiles
        start = pl.multiple_of((step % tiles) * TILE, TILE)
        q = q_s[r, pl.ds(start, TILE), :]
        none = jnp.zeros_like(q)
        stacked = jnp.concatenate(
            [jnp.where(lane_head == h, q, none) for h in range(heads)], axis=0
        )
        k = k_s[pl.ds(r, reach), pl.ds(start, SPAN), :].reshape(keys, width)
        v = v_s[pl.ds(r, reach), pl.ds(start, SPAN), :].reshape(keys, width)
        scores = dot_nt(stacked, k)
        row = key_row + (place_ref[0] + r)
        col = key_col + start
        ok = band & (row >= 0) & (row < total_rows) & (col >= 0) & (col < cols)
        bias = jnp.where(ok, 0.0, FAR)
        mixed = jnp.zeros((TILE, width), F32)
        weights = []
        totals = []
        for h in range(heads):
            part = scores[h * TILE : (h + 1) * TILE] * scale_ref[h] + bias
            weight = jnp.exp(part)
            totals.append(jnp.sum(weight, axis=1, keepdims=True))
            weights.append(weight.astype(BF16))
        summed = dot(jnp.concatenate(weights, axis=0), v)
        for h in range(heads):
            mixed = mixed + jnp.where(
                lane_head == h, summed[h * TILE : (h + 1) * TILE] / totals[h], 0.0
            )
        mix_s[r, pl.ds(start, TILE), :] = mixed.astype(BF16)
        return carry

    lax.fori_loop(0, rows * tiles, one_tile, 0)

    hidden_count = mlp_out_ref.shape[0]
    for r in range(rows):
        stream = own_ref[r].astype(F32) + dot(mix_s[r], out_w_ref[...])
        normed = rms_scale(stream, gain_mlp_ref[...]).astype(BF16)
        lifted = dot(normed, mlp_in_ref[...])
        hidden = (
            jax.nn.gelu(lifted[:, :hidden_count], approximate=True) * lifted[:, hidden_count:]
        ).astype(BF16)
        level = (stream + dot(hidden, mlp_out_ref[...])).astype(BF16)
        level_ref[r] = level
        row_s[...] = level.astype(F32).reshape(cols, width // 128, 128)
        for j in range(2):
            at = ((r % 2) * 2 + j) * width
            for g in range(width // 128):
                flat_ref[r // 2, :, pl.ds(at + g * 128, 128)] = row_s[
                    pl.ds(j, cols // 2, stride=2), g, :
                ].astype(BF16)


def merge_body(flat_ref, weight_ref, out_ref, row_s):
    rows, cols, _ = flat_ref.shape
    depth = weight_ref.shape[1]
    for i in range(rows):
        level = dot(flat_ref[i], weight_ref[...]).astype(BF16)
        row_s[...] = level.astype(F32).reshape(cols, depth // 128, 128)
        for j in range(2):
            at = (i * 2 + j) * depth
            for g in range(depth // 128):
                out_ref[:, pl.ds(at + g * 128, 128)] = row_s[
                    pl.ds(j, cols // 2, stride=2), g, :
                ].astype(BF16)


def coarse_body(low_ref, high_ref, pack_ref, out_ref):
    weight = pack_ref[:, :, :256].reshape(2048, 256)
    low = low_ref[...].reshape(256, 1024)
    high = high_ref[...].reshape(256, 1024)
    out_ref[...] = (dot(low, weight[:1024]) + dot(high, weight[1024:])).astype(BF16)


def qkv_body(parts_ref, gain_ref, pack_ref, time_ref, space_ref):
    value = jnp.concatenate([parts_ref[i] for i in range(4)], axis=1).astype(F32)
    normed = rms_scale(value, gain_ref[...]).astype(BF16)
    sums = head_sums(384)
    lane = lax.broadcasted_iota(jnp.int32, (256, 384), 1) // HEAD
    for h in range(2):
        weight = pack_ref[:, h * 64 : (h + 1) * 64, 256:640].reshape(1024, 384)
        packed = dot(normed, weight).astype(BF16)
        wide = packed.astype(F32)
        unit = jnp.where(lane % 3 == 2, wide, unit_heads(wide, sums)).astype(BF16)
        time_ref[:, pl.ds(h * 384, 384)] = unit
        space_ref[2 * h] = unit[:, :192]
        space_ref[2 * h + 1] = unit[:, 192:]


def time_body(scale_ref, packed_ref, out_ref):
    packed = packed_ref[...].reshape(256, 768)
    same = (
        lax.broadcasted_iota(jnp.int32, (256, 256), 0) % 16
        == lax.broadcasted_iota(jnp.int32, (256, 256), 1) % 16
    )
    bias = jnp.where(same, 0.0, FAR)
    results = []
    for h in range(4):
        part = packed[:, h * 192 : (h + 1) * 192]
        weight = jnp.exp(dot_nt(part[:, :64], part[:, 64:128]) * scale_ref[h] + bias)
        total = jnp.sum(weight, axis=1, keepdims=True)
        results.append(dot(weight.astype(BF16), part[:, 128:]) / total)
    out_ref[...] = jnp.concatenate(results, axis=1).astype(BF16).reshape(16, 16, 256)


def space_body(scale_ref, packed_ref, out_ref):
    k = packed_ref[:, :, 64:128].reshape(1024, 64)
    v = packed_ref[:, :, 128:192].reshape(1024, 64)
    for i in range(4):
        q = packed_ref[i, :, :64]
        weight = jnp.exp(dot_nt(q, k) * scale_ref[0])
        total = jnp.sum(weight, axis=1, keepdims=True)
        out_ref[i] = (dot(weight.astype(BF16), v) / total).astype(BF16)


def finish_body(
    core_ref,
    time_ref,
    space_ref,
    coarse_ref,
    mine_ref,
    other_ref,
    last_ref,
    one_ref,
    lerp_two_ref,
    level_ref,
    lerp_one_ref,
    out_ref,
    row_s,
):
    first = core_ref[0] == 0
    attended = [time_ref[g] for g in range(4)] + [space_ref[g] for g in range(4)]
    attended = jnp.concatenate(attended, axis=1)

    def halves(product):
        a = product(mine_ref)
        b = product(other_ref)
        return jnp.concatenate([jnp.where(first, a, b), jnp.where(first, b, a)], axis=1)

    def mixed(ref):
        return jnp.concatenate(
            [dot(attended, ref[y, :, :, :128].reshape(2048, 128)) for y in range(4)], axis=1
        )

    coarse = jnp.concatenate([coarse_ref[g] for g in range(4)], axis=1).astype(F32)
    coarse = (coarse + halves(mixed)).astype(BF16)

    def raised(ref):
        return jnp.concatenate(
            [
                dot(coarse, ref[y, :, h * 64 : (h + 1) * 64, 128:256].reshape(1024, 128))
                for y in range(4)
                for h in range(2)
            ],
            axis=1,
        )

    raised_two = halves(raised)
    skip = one_ref[...].astype(F32)
    lerp = jnp.concatenate([lerp_two_ref[...]] * 4, axis=1)
    blended = (skip + lerp * (raised_two - skip)).astype(BF16)
    stacked = jnp.concatenate([blended[:, p * 512 : (p + 1) * 512] for p in range(4)], axis=0)
    lerp_one = lerp_one_ref[...]
    weights = [
        last_ref[:, q * 32 : (q + 1) * 32, 256:512].reshape(512, 256) for q in range(4)
    ]
    cols = level_ref.shape[1]
    products = [dot(stacked, w) for w in weights]
    for i in range(2):
        for i2 in range(2):
            for j in range(2):
                for j2 in range(2):
                    p = i * 2 + j
                    tile = products[i2 * 2 + j2][p * 64 : (p + 1) * 64]
                    for g in range(2):
                        row_s[pl.ds(2 * j + j2, cols // 4, stride=4), g, :] = tile[
                            :, g * 128 : (g + 1) * 128
                        ]
            r = 2 * i + i2
            new = row_s[...].reshape(cols, 256)
            old = level_ref[r].astype(F32)
            out_ref[r] = (old + lerp_one * (new - old)).astype(BF16)


def sent_to_all(shard, axis):
    length = lax.axis_size(axis)
    return lax.all_to_all(
        jnp.broadcast_to(shard[None], (length, *shard.shape)), axis, 0, 0, tiled=True
    )


def rows_of(shard):
    for axis in ("zl", "x"):
        tiles = sent_to_all(shard, axis)
        shard = tiles.reshape(-1, shard.shape[1])
    return shard


def columns(shard, index, count):
    width = shard.shape[1] // count
    return lax.dynamic_slice_in_dim(shard, index * width, width, axis=1)


def stack_columns(shard, count):
    width = shard.shape[1] // count
    return jnp.concatenate([shard[:, i * width : (i + 1) * width] for i in range(count)], axis=0)


def shards(
    tokens,
    gain_attn,
    fine_qkv,
    fine_scale,
    fine_out,
    gain_mlp,
    mlp_in,
    mlp_out,
    merge_one,
    merge_two,
    coarse_gain,
    coarse_qkv,
    time_scale,
    space_scale,
    coarse_out,
    split_two,
    lerp_two,
    split_one,
    lerp_one,
):
    own = tokens[0]
    rows, cols, width = own.shape
    slab = lax.axis_index(BA)
    slabs = lax.axis_size(BA)
    above = lax.ppermute(own[rows - HALO :], BA, [(i, i + 1) for i in range(slabs - 1)])
    below = lax.ppermute(own[:HALO], BA, [(i + 1, i) for i in range(slabs - 1)])

    core = lax.axis_index("c")
    quarter = lax.axis_index(GROUP)
    part = core * 4 + lax.axis_index(Y)
    one_all = rows_of(merge_one)
    second = rows_of(
        jnp.concatenate(
            [columns(merge_two, quarter, 4), stack_columns(columns(coarse_qkv, quarter, 4), 2)],
            axis=1,
        )
    ).reshape(16, 128, 640)
    third = rows_of(
        jnp.concatenate(
            [
                columns(coarse_out, part, 8),
                stack_columns(columns(split_two, part, 8), 2),
                stack_columns(split_one, 4),
            ],
            axis=1,
        )
    )
    mine = sent_to_all(third[:, :256], Y).reshape(4, 16, 128, 256)
    other = lax.ppermute(mine, "c", [(0, 1), (1, 0)])
    third = third.reshape(16, 128, 512)

    place = jnp.stack([slab * rows, slabs * rows]).astype(jnp.int32)
    padded = cols + 2 * PAD
    level_zero, flat_one = call(
        fine_body,
        (
            jax.ShapeDtypeStruct((rows, cols, width), BF16),
            jax.ShapeDtypeStruct((rows // 2, cols // 2, 4 * width), BF16),
        ),
        [
            pltpu.VMEM((rows, cols, width), BF16),
            pltpu.VMEM((rows + 2 * HALO, padded, width), BF16),
            pltpu.VMEM((rows + 2 * HALO, padded, width), BF16),
            pltpu.VMEM((rows, cols, width), BF16),
            pltpu.VMEM((cols, width // 128, 128), F32),
        ],
        smem=2,
        count=11,
    )(
        place,
        fine_scale / HEAD,
        own,
        above,
        below,
        gain_attn[None],
        fine_qkv,
        fine_out,
        gain_mlp[None],
        mlp_in,
        mlp_out,
    )
    flat_two = call(
        merge_body,
        jax.ShapeDtypeStruct((cols // 4, 2048), BF16),
        [pltpu.VMEM((cols // 2, 4, 128), F32)],
        count=2,
    )(flat_one, one_all)
    low = lax.all_gather(flat_two[:, :1024], GROUP, axis=0)
    high = lax.all_gather(flat_two[:, 1024:], GROUP, axis=0)
    coarse_part = call(coarse_body, jax.ShapeDtypeStruct((256, 256), BF16), count=3)(
        low, high, second
    )
    coarse_parts = lax.all_gather(coarse_part, GROUP, axis=0)
    for_time, for_space = call(
        qkv_body,
        (jax.ShapeDtypeStruct((256, 768), BF16), jax.ShapeDtypeStruct((4, 256, 192), BF16)),
        count=3,
    )(coarse_parts, coarse_gain[None], second)
    time_in = lax.all_to_all(for_time.reshape(16, 16, 768), AA, 0, 0, tiled=True)
    space_in = lax.all_to_all(for_space, ACROSS, 0, 0, tiled=True)
    head = quarter * 4 + lax.axis_index(ACROSS)
    space_out = call(
        space_body, jax.ShapeDtypeStruct((4, 256, 64), BF16), smem=1, count=2
    )(lax.dynamic_slice_in_dim(space_scale / HEAD, head, 1), space_in)
    space_back = lax.all_to_all(space_out, ACROSS, 0, 0, tiled=True)
    time_out = call(time_body, jax.ShapeDtypeStruct((16, 16, 256), BF16), smem=1, count=2)(
        lax.dynamic_slice_in_dim(time_scale / HEAD, quarter * 4, 4), time_in
    )
    time_back = lax.all_to_all(time_out, AA, 0, 0, tiled=True)
    both = jnp.concatenate(
        [
            time_back.reshape(4, 64, 256),
            space_back.reshape(4, 4, 64, 64).transpose(1, 2, 0, 3).reshape(4, 64, 256),
        ],
        axis=2,
    )
    both = lax.all_to_all(both, GROUP, 0, 0, tiled=True)
    own_coarse = lax.dynamic_slice_in_dim(coarse_parts, quarter * 64, 64, axis=1)
    refined = call(
        finish_body,
        jax.ShapeDtypeStruct((rows, cols, width), BF16),
        [pltpu.VMEM((cols, 2, 128), F32)],
        smem=1,
        count=11,
    )(
        core.reshape(1).astype(jnp.int32),
        both[:, :, :256],
        both[:, :, 256:],
        own_coarse,
        mine,
        other,
        third,
        flat_two,
        lerp_two[None],
        level_zero,
        lerp_one[None],
    )
    return refined[None]


def solution(mesh):
    torus = Mesh(
        mesh.devices.reshape(4, 4, 2, 2, 2, 2), ("x", "zl", "zh", "yh", "yl", "c")
    )
    return jax.shard_map(
        shards,
        mesh=torus,
        in_specs=(
            P(AA, BA, None, None),
            P(),
            P(),
            P(),
            P(),
            P(),
            P(),
            P(),
            P(AA, None),
            P(AA, None),
            P(),
            P(AA, None),
            P(),
            P(),
            P(AA, None),
            P(AA, None),
            P(),
            P(AA, None),
            P(),
        ),
        out_specs=P(AA, BA, None, None),
        check_vma=False,
    )
```

time: 518 us -> 323 us (0.62); the launches traced: 507 us -> 321 us
  waiting for transfers between devices: 348 us -> 55.6 us
  blocking collectives: 0 us -> 145 us
  Pallas kernels: 0 us -> 41.8 us
  other arithmetic: 39.7 us -> 1.99 us
  matrix products: 26.2 us -> 0 us
  between operations: 15.8 us -> 0.25 us
  local copies, waits for them, and re-layouts: 35.5 us -> 20.5 us
  starting transfers between devices: 41.7 us -> 55.8 us
    all_gather x5 -> x0, waiting for transfers between devices: 286 us -> none  [the longest x1 129 us: shards(): whole_qkv = lax.all_gather(coarse_qkv, AA, axis=0, tiled=True)]
    all_to_all x0 -> x4, blocking collectives: none -> 120 us  [the longest x3 95.5 us: sent_to_all(): lax.all_to_all(jnp.broadcast_to(shard[None], (length, *shard.shape)), axi...]
    pallas_call x0 -> x7, Pallas kernels: none -> 41.8 us  [the longest x1 17.1 us: shards(): call(fine_body, (jax.ShapeDtypeStruct((rows, cols, width), BF16), jax.Sha...]
    dot_general x17 -> x0, matrix products: 26.2 us -> none  [the longest x4 10.3 us: row_product(): return jnp.dot(operand, weight_rows, preferred_element_type=jnp.float32)]
    all_gather x0 -> x3, blocking collectives: none -> 25.3 us  [the longest x1 8.84 us: shards(): high = lax.all_gather(flat_two[:, 1024:], GROUP, axis=0)]
    convert_element_type x16 -> x0, other arithmetic: 16.8 us -> none  [the longest x1 10.3 us: finish_fine(): attended.transpose(2, 3, 0, 1).reshape(row_count * col_count, width)]
    reduce_sum x11 -> x0, other arithmetic: 15.3 us -> none  [the longest x3 11.2 us: window_attention(): scores = jnp.sum(query_wide * key_part, axis=1) * factor]
    all_to_all x4, waiting for transfers between devices: 32.7 us -> 22.3 us  [the longest x1 6.83 us: shards(): time_back = lax.all_to_all(time_out, AA, 0, 0, tiled=True)]
  transfers between devices with their start and end apart: 13 -> 11, of which waited for: 10 -> 9; matrix products, arithmetic and copies ran while one was open for 17% -> 5% of each run, Pallas kernels for 0% -> 11%
where the time goes in v1:
time: 323 us; the launch traced here: 321 us
  blocking collectives  145 us (45%)
  starting transfers between devices  55.8 us (17%)
  waiting for transfers between devices  55.6 us (17%)
  Pallas kernels  41.8 us (13%)
  local copies, waits for them, and re-layouts  20.5 us (6%)
    all_to_all x3, blocking collectives, sent_to_all(): lax.all_to_all(jnp.broadcast_to(shard[None], (length, *shard.shape)), axi...  95.5 us
    all_to_all x4, waiting for transfers between devices, sent_to_all(): lax.all_to_all(jnp.broadcast_to(shard[None], (length, *shard.shape)), axi...  29.6 us
    all_to_all x1, blocking collectives, shards(): space_in = lax.all_to_all(for_space, ACROSS, 0, 0, tiled=True)  24.5 us
    all_to_all x4, starting transfers between devices, sent_to_all(): lax.all_to_all(jnp.broadcast_to(shard[None], (length, *shard.shape)), axi...  17.9 us
    pallas_call x1, Pallas kernels, shards(): call(fine_body, (jax.ShapeDtypeStruct((rows, cols, width), BF16), jax.Sha...  17.1 us
    all_to_all x1, starting transfers between devices, shards(): lax.all_to_all(for_time.reshape(16, 16, 768), AA, 0, 0, tiled=True)  12.6 us
    all_gather x1, blocking collectives, shards(): high = lax.all_gather(flat_two[:, 1024:], GROUP, axis=0)  8.84 us
    all_gather x1, blocking collectives, shards(): coarse_parts = lax.all_gather(coarse_part, GROUP, axis=0)  8.74 us
  transfers between devices with their start and end apart: 11, of which 9 were waited for; matrix products, arithmetic and copies ran while one was open for 5% of the time, Pallas kernels for 11%

profile of v1, /device:TPU:1, one launch (start us, length us, event | category | flops | bytes accessed | tf_op | source)
XLA Modules:
  0.0 321.2 jit_solution(7012784625572201452)
XLA Ops:
  1.6 6.4 %all-to-all-start = ((bf16[4,64,512]{2,1,0:T(8,128)(2,1)}), bf16[4,64,512]{2,1,0:T(8,128)(2,1)S(1)}, u32[]{:S(2)}, u32[]{:S(2)}) async-start(bf16[4,64,512]{2,1,0:T(8,128)(2,1)} %broadcast_in_dim.65), calls=%async_computation | async-start | bytes 524288 | tf_op jit(solution)/shard_map/all_to_all | solution.py:307
  10.3 5.3 %all-to-all-done = bf16[4,64,512]{2,1,0:T(8,128)(2,1)S(1)} async-done(((bf16[4,64,512]{2,1,0:T(8,128)(2,1)}), bf16[4,64,512]{2,1,0:T(8,128)(2,1)S(1)}, u32[]{:S(2)}, u32[]{:S(2)}) %all-to-all-start) | async-done | bytes 262176 | tf_op jit(solution)/shard_map/all_to_all | solution.py:307
  20.8 12.7 %all-to-all-done.9 = bf16[4,128,512]{2,1,0:T(8,128)(2,1)S(1)} async-done(((bf16[4,128,512]{2,1,0:T(8,128)(2,1)}), bf16[4,128,512]{2,1,0:T(8,128)(2,1)S(1)}, u32[]{:S(2)}, u32[]{:S(2)}) %all-to-all-start.9) | async-done | bytes 524320 | tf_op jit(solution)/shard_map/all_to_all | solution.py:307
  33.6 19.4 %all_to_all.60 = bf16[4,128,640]{2,1,0:T(8,128)(2,1)} all-to-all(bf16[4,128,640]{2,1,0:T(8,128)(2,1)S(1)} %broadcast_in_dim.68), channel_id=1, replica_groups=mesh['x'=4,'zl'=4,'zh'=2,'yh'=2,'yl'=2,'c'=2] {'zl'}, dimensions={0} | all-to-all | bytes 1310720 | tf_op jit(solution)/shard_map/all_to_all | solution.py:307
  53.2 27.8 %all_to_all.61 = bf16[4,512,512]{2,1,0:T(8,128)(2,1)S(1)} all-to-all(bf16[4,512,512]{2,1,0:T(8,128)(2,1)S(1)} %broadcast_in_dim.74), channel_id=1, replica_groups=mesh['x'=4,'zl'=4,'zh'=2,'yh'=2,'yl'=2,'c'=2] {'x'}, dimensions={0} | all-to-all | bytes 4194304 | tf_op jit(solution)/shard_map/all_to_all | solution.py:307
  82.1 4.2 %all-to-all-start.1 = ((bf16[4,256,512]{2,1,0:T(8,128)(2,1)}), bf16[4,256,512]{2,1,0:T(8,128)(2,1)}, u32[]{:S(2)}, u32[]{:S(2)}) async-start(bf16[4,256,512]{2,1,0:T(8,128)(2,1)} %broadcast_in_dim.67), calls=%async_computation.1 | async-start | bytes 2097152 | tf_op jit(solution)/shard_map/all_to_all | solution.py:307
  86.5 11.5 %all-to-all-done.1 = bf16[4,256,512]{2,1,0:T(8,128)(2,1)} async-done(((bf16[4,256,512]{2,1,0:T(8,128)(2,1)}), bf16[4,256,512]{2,1,0:T(8,128)(2,1)}, u32[]{:S(2)}, u32[]{:S(2)}) %all-to-all-start.1) | async-done | bytes 1048608 | tf_op jit(solution)/shard_map/all_to_all | solution.py:307
  98.3 48.4 %all_to_all.62 = bf16[4,2048,256]{2,1,0:T(8,128)(2,1)} all-to-all(bf16[4,2048,256]{2,1,0:T(8,128)(2,1)S(1)} %broadcast_in_dim.75), channel_id=1, replica_groups=mesh['x'=4,'zl'=4,'zh'=2,'yh'=2,'yl'=2,'c'=2] {'yh','yl'}, dimensions={0} | all-to-all | bytes 8388608 | tf_op jit(solution)/shard_map/all_to_all | solution.py:307
  148.4 3.8 %all-to-all-start.3 = ((bf16[4,512,640]{2,1,0:T(8,128)(2,1)}), bf16[4,512,640]{2,1,0:T(8,128)(2,1)S(1)}, u32[]{:S(2)}, u32[]{:S(2)}) async-start(bf16[4,512,640]{2,1,0:T(8,128)(2,1)} %broadcast_in_dim.70), calls=%async_computation.3 | async-start | bytes 5242880 | tf_op jit(solution)/shard_map/all_to_all | solution.py:307
  152.2 5.7 %collective-permute-start.2 = (bf16[4,16,128,256]{3,2,1,0:T(8,128)(2,1)}, bf16[4,16,128,256]{3,2,1,0:T(8,128)(2,1)}, u32[]{:S(2)}, u32[]{:S(2)}) collective-permute-start(bf16[4,16,128,256]{3,2,1,0:T(8,128)(2,1)} %bitcast.31), channel_id=1, source_target_pairs={{0,1},{1,0},{2,3},{3,2},{4,5},{5,4},{6,7},{7,6},{8,9},{9,8},{10,11... | collective-permute-start | bytes 12582920 | tf_op jit(solution)/shard_map/ppermute | solution.py:378
  160.8 3.6 %collective-permute-start = (bf16[3,256,256]{2,1,0:T(8,128)(2,1)}, bf16[3,256,256]{2,1,0:T(8,128)(2,1)}, u32[]{:S(2)}, u32[]{:S(2)}) collective-permute-start(bf16[3,256,256]{2,1,0:T(8,128)(2,1)} %get-tuple-element.14), channel_id=1, source_target_pairs={{0,1},{1,2},{2,3},{3,4},{4,5},{5,6},{6,7},{7,8},{8,9},{9,10},{10,1... | collective-permute-start | bytes 1179656 | tf_op jit(solution)/shard_map/ppermute | solution.py:354
  169.4 17.1 %shard_map.181 = (bf16[4,256,256]{2,1,0:T(8,128)(2,1)}, bf16[2,128,1024]{2,1,0:T(8,128)(2,1)}) custom-call(s32[2]{0:T(128)} %pad_add_fusion.place_ref, f32[4]{0:T(128)} %broadcast_multiply_fusion.scale_ref, bf16[4,256,256]{2,1,0:T(8,128)(2,1)} %bitcast.35, bf16[3,256,256]{2,1,0:T(8,128)(2,1)} %collective-permute-done.above_ref, ...), custom_call_target="tpu_custom_call" | custom-call | tf_op jit(solution)/shard_map/pallas_call | solution.py:383
  190.5 8.8 %all-gather.1 = bf16[256,1024]{1,0:T(8,128)(2,1)} all-gather(bf16[64,1024]{1,0:T(8,128)(2,1)S(1)} %get-tuple-element.21), channel_id=3, replica_groups=mesh['x'=4,'zl'=4,'zh'=2,'yh'=2,'yl'=2,'c'=2] {'yl','c'}, dimensions={0}, use_global_device_ids=true | all-gather | bytes 655360 | tf_op jit(solution)/shard_map/all_gather | solution.py:418
  199.4 7.7 %all-gather = bf16[256,1024]{1,0:T(8,128)(2,1)} all-gather(bf16[64,1024]{1,0:T(8,128)(2,1)S(1)} %get-tuple-element.22), channel_id=2, replica_groups=mesh['x'=4,'zl'=4,'zh'=2,'yh'=2,'yl'=2,'c'=2] {'yl','c'}, dimensions={0}, use_global_device_ids=true | all-gather | bytes 655360 | tf_op jit(solution)/shard_map/all_gather | solution.py:417
  211.8 8.7 %all-gather.2 = bf16[1024,256]{1,0:T(8,128)(2,1)} all-gather(bf16[256,256]{1,0:T(8,128)(2,1)} %shard_map.183), channel_id=4, replica_groups=mesh['x'=4,'zl'=4,'zh'=2,'yh'=2,'yl'=2,'c'=2] {'yl','c'}, dimensions={0}, use_global_device_ids=true | all-gather | bytes 655360 | tf_op jit(solution)/shard_map/all_gather | solution.py:422
  220.5 4.3 %shard_map.184 = (bf16[256,768]{1,0:T(8,128)(2,1)}, bf16[4,256,192]{2,1,0:T(8,128)(2,1)}) custom-call(bf16[4,256,256]{2,1,0:T(8,128)(2,1)} %bitcast.36, f32[1,1024]{1,0:T(1,128)} %bitcast.46, bf16[16,128,640]{2,1,0:T(8,128)(2,1)} %bitcast.30), custom_call_target="tpu_custom_call" | custom-call | tf_op jit(solution)/shard_map/pallas_call | solution.py:423
  226.1 24.5 %all_to_all.63 = bf16[4,256,192]{1,2,0:T(8,128)(2,1)S(1)} all-to-all(bf16[4,256,192]{1,2,0:T(8,128)(2,1)S(1)} %copy.21), channel_id=1, replica_groups=mesh['x'=4,'zl'=4,'zh'=2,'yh'=2,'yl'=2,'c'=2] {'zh','yh'}, dimensions={0} | all-to-all | bytes 786432 | tf_op jit(solution)/shard_map/all_to_all | solution.py:429
  250.6 12.6 %all-to-all-start.4 = ((bf16[16,16,768]{2,1,0:T(8,128)(2,1)}), bf16[16,16,768]{2,1,0:T(8,128)(2,1)S(1)}, u32[]{:S(2)}, u32[]{:S(2)}) async-start(bf16[16,16,768]{2,1,0:T(8,128)(2,1)} %bitcast.45), calls=%async_computation.4 | async-start | bytes 786432 | tf_op jit(solution)/shard_map/all_to_all | solution.py:428
  264.8 3.8 %shard_map.186 = bf16[4,256,64]{2,1,0:T(8,128)(2,1)} custom-call(f32[1]{0:T(128)} %dynamic_slice.24.scale_ref, bf16[4,256,192]{2,1,0:T(8,128)(2,1)} %copy.22.packed_ref), custom_call_target="tpu_custom_call" | custom-call | tf_op jit(solution)/shard_map/pallas_call | solution.py:431
  270.4 5.7 %all-to-all-done.4.packed_ref = bf16[16,16,768]{2,1,0:T(8,128)(2,1)S(1)} async-done(((bf16[16,16,768]{2,1,0:T(8,128)(2,1)}), bf16[16,16,768]{2,1,0:T(8,128)(2,1)S(1)}, u32[]{:S(2)}, u32[]{:S(2)}) %all-to-all-start.4) | async-done | bytes 393248 | tf_op jit(solution)/shard_map/all_to_all | solution.py:428
  282.5 6.2 %all-to-all-done.7 = bf16[4,256,64]{1,2,0:T(8,128)(2,1)S(1)} async-done(((bf16[4,256,64]{1,2,0:T(8,128)(2,1)}), bf16[4,256,64]{1,2,0:T(8,128)(2,1)S(1)}, u32[]{:S(2)}, u32[]{:S(2)}) %all-to-all-start.7) | async-done | bytes 131104 | tf_op jit(solution)/shard_map/all_to_all | solution.py:434
  292.7 6.8 %all-to-all-done.5 = bf16[16,16,256]{2,1,0:T(8,128)(2,1)S(1)} async-done(((bf16[16,16,256]{2,1,0:T(8,128)(2,1)}), bf16[16,16,256]{2,1,0:T(8,128)(2,1)S(1)}, u32[]{:S(2)}, u32[]{:S(2)}) %all-to-all-start.5) | async-done | bytes 131104 | tf_op jit(solution)/shard_map/all_to_all | solution.py:438
  300.3 7.2 %all-to-all-start.8 = ((bf16[4,64,512]{2,1,0:T(8,128)(2,1)}), bf16[4,64,512]{2,1,0:T(8,128)(2,1)S(1)}, u32[]{:S(2)}, u32[]{:S(2)}) async-start(bf16[4,64,512]{2,1,0:T(8,128)(2,1)} %pad_maximum_fusion), calls=%async_computation.8 | async-start | bytes 524288 | tf_op jit(solution)/shard_map/all_to_all | solution.py:446
  313.3 7.9 %shard_map.187 = bf16[4,256,256]{2,1,0:T(8,128)(2,1)} custom-call(s32[1]{0:T(128)} %bitcast.core_ref, bf16[4,64,256]{2,1,0:T(8,128)(2,1)} %get-tuple-element.20.time_ref, bf16[4,64,256]{2,1,0:T(8,128)(2,1)} %get-tuple-element.19.space_ref, bf16[4,64,256]{2,1,0:T(8,128)(2,1)} %constant_dynamic-slice_fusion.4.coarse_ref, bf16[4,16,128,256]{3,2,1,0:T(8,128)(2,1)} %bitcast.32, ...), custom_call_target="tpu_custom_call" | custom-call | tf_op jit(solution)/shard_map/pallas_call | solution.py:448
  (63 shorter events, 50.6 us)
Async XLA Ops:
  0.0 19.9 %copy-start = (bf16[128,1024]{1,0:T(8,128)(2,1)S(1)}, bf16[128,1024]{1,0:T(8,128)(2,1)}, u32[]{:S(2)}) copy-start(bf16[128,1024]{1,0:T(8,128)(2,1)} %param.28) | copy-start | bytes 786436
  1.6 14.0 %all-to-all-start = ((bf16[4,64,512]{2,1,0:T(8,128)(2,1)}), bf16[4,64,512]{2,1,0:T(8,128)(2,1)S(1)}, u32[]{:S(2)}, u32[]{:S(2)}) async-start(bf16[4,64,512]{2,1,0:T(8,128)(2,1)} %broadcast_in_dim.65), calls=%async_computation | async-start | bytes 524288 | tf_op jit(solution)/shard_map/all_to_all | solution.py:307
  16.4 17.1 %all-to-all-start.9 = ((bf16[4,128,512]{2,1,0:T(8,128)(2,1)}), bf16[4,128,512]{2,1,0:T(8,128)(2,1)S(1)}, u32[]{:S(2)}, u32[]{:S(2)}) async-start(bf16[4,128,512]{2,1,0:T(8,128)(2,1)} %broadcast_in_dim.72), calls=%async_computation.9 | async-start | bytes 1048576 | tf_op jit(solution)/shard_map/all_to_all | solution.py:307
  81.0 5.5 %copy-start.2 = (bf16[4,512,512]{2,1,0:T(8,128)(2,1)}, bf16[4,512,512]{2,1,0:T(8,128)(2,1)S(1)}, u32[]{:S(2)}) copy-start(bf16[4,512,512]{2,1,0:T(8,128)(2,1)S(1)} %all_to_all.61) | copy-start | bytes 6291460
  82.1 15.9 %all-to-all-start.1 = ((bf16[4,256,512]{2,1,0:T(8,128)(2,1)}), bf16[4,256,512]{2,1,0:T(8,128)(2,1)}, u32[]{:S(2)}, u32[]{:S(2)}) async-start(bf16[4,256,512]{2,1,0:T(8,128)(2,1)} %broadcast_in_dim.67), calls=%async_computation.1 | async-start | bytes 2097152 | tf_op jit(solution)/shard_map/all_to_all | solution.py:307
  98.3 48.4 %copy-start.4 = (bf16[4,128,640]{2,1,0:T(8,128)(2,1)S(1)}, bf16[4,128,640]{2,1,0:T(8,128)(2,1)}, u32[]{:S(2)}) copy-start(bf16[4,128,640]{2,1,0:T(8,128)(2,1)} %all_to_all.60) | copy-start | bytes 1966084
  148.4 9.5 %copy-start.3 = (bf16[1,4,256,256]{3,2,1,0:T(8,128)(2,1)S(1)}, bf16[1,4,256,256]{3,2,1,0:T(8,128)(2,1)}, u32[]{:S(2)}) copy-start(bf16[1,4,256,256]{3,2,1,0:T(8,128)(2,1)} %param.19) | copy-start | bytes 1572868
  148.4 16.7 %copy-start.7 = (f32[4]{0:T(128)S(1)}, f32[4]{0:T(128)}, u32[]{:S(2)}) copy-start(f32[4]{0:T(128)} %param.22) | copy-start | bytes 52
  148.4 58.7 %all-to-all-start.3 = ((bf16[4,512,640]{2,1,0:T(8,128)(2,1)}), bf16[4,512,640]{2,1,0:T(8,128)(2,1)S(1)}, u32[]{:S(2)}, u32[]{:S(2)}) async-start(bf16[4,512,640]{2,1,0:T(8,128)(2,1)} %broadcast_in_dim.70), calls=%async_computation.3 | async-start | bytes 5242880 | tf_op jit(solution)/shard_map/all_to_all | solution.py:307
  152.2 161.1 %collective-permute-start.2 = (bf16[4,16,128,256]{3,2,1,0:T(8,128)(2,1)}, bf16[4,16,128,256]{3,2,1,0:T(8,128)(2,1)}, u32[]{:S(2)}, u32[]{:S(2)}) collective-permute-start(bf16[4,16,128,256]{3,2,1,0:T(8,128)(2,1)} %bitcast.31), channel_id=1, source_target_pairs={{0,1},{1,0},{2,3},{3,2},{4,5},{5,4},{6,7},{7,6},{8,9},{9,8},{10,11... | collective-permute-start | bytes 12582920 | tf_op jit(solution)/shard_map/ppermute | solution.py:378
  158.8 9.6 %collective-permute-start.1 = (bf16[3,256,256]{2,1,0:T(8,128)(2,1)}, bf16[3,256,256]{2,1,0:T(8,128)(2,1)S(1)}, u32[]{:S(2)}, u32[]{:S(2)}) collective-permute-start(bf16[3,256,256]{2,1,0:T(8,128)(2,1)} %get-tuple-element.13), channel_id=1, source_target_pairs={{1,0},{2,1},{3,2},{4,3},{5,4},{6,5},{7,6},{8,7},{9,8},{10,9},{11,1... | collective-permute-start | bytes 1179656 | tf_op jit(solution)/shard_map/ppermute | solution.py:355
  160.8 8.7 %collective-permute-start = (bf16[3,256,256]{2,1,0:T(8,128)(2,1)}, bf16[3,256,256]{2,1,0:T(8,128)(2,1)}, u32[]{:S(2)}, u32[]{:S(2)}) collective-permute-start(bf16[3,256,256]{2,1,0:T(8,128)(2,1)} %get-tuple-element.14), channel_id=1, source_target_pairs={{0,1},{1,2},{2,3},{3,4},{4,5},{5,6},{6,7},{7,8},{8,9},{9,10},{10,1... | collective-permute-start | bytes 1179656 | tf_op jit(solution)/shard_map/ppermute | solution.py:354
  168.4 1.0 copy-start.6
  207.1 1.5 copy-start.1
  220.5 42.6 %copy-start.8 = (f32[16]{0:T(128)S(1)}, f32[16]{0:T(128)}, u32[]{:S(2)}) copy-start(f32[16]{0:T(128)} %param.32) | copy-start | bytes 196
  224.8 54.6 %copy-start.9 = (f32[16]{0:T(128)S(1)}, f32[16]{0:T(128)}, u32[]{:S(2)}) copy-start(f32[16]{0:T(128)} %param.31) | copy-start | bytes 196
  250.6 25.5 %all-to-all-start.4 = ((bf16[16,16,768]{2,1,0:T(8,128)(2,1)}), bf16[16,16,768]{2,1,0:T(8,128)(2,1)S(1)}, u32[]{:S(2)}, u32[]{:S(2)}) async-start(bf16[16,16,768]{2,1,0:T(8,128)(2,1)} %bitcast.45), calls=%async_computation.4 | async-start | bytes 786432 | tf_op jit(solution)/shard_map/all_to_all | solution.py:428
  276.1 4.0 %copy-start.5 = (bf16[16,16,768]{2,1,0:T(8,128)(2,1)}, bf16[16,16,768]{2,1,0:T(8,128)(2,1)S(1)}, u32[]{:S(2)}) copy-start(bf16[16,16,768]{2,1,0:T(8,128)(2,1)S(1)} %all-to-all-done.4.packed_ref) | copy-start | bytes 1179652
  276.1 12.7 %all-to-all-start.7 = ((bf16[4,256,64]{1,2,0:T(8,128)(2,1)}), bf16[4,256,64]{1,2,0:T(8,128)(2,1)S(1)}, u32[]{:S(2)}, u32[]{:S(2)}) async-start(bf16[4,256,64]{1,2,0:T(8,128)(2,1)} %copy.23), calls=%async_computation.7 | async-start | bytes 262144 | tf_op jit(solution)/shard_map/all_to_all | solution.py:434
  288.8 10.8 %all-to-all-start.5 = ((bf16[16,16,256]{2,1,0:T(8,128)(2,1)}), bf16[16,16,256]{2,1,0:T(8,128)(2,1)S(1)}, u32[]{:S(2)}, u32[]{:S(2)}) async-start(bf16[16,16,256]{2,1,0:T(8,128)(2,1)} %shard_map.185), calls=%async_computation.5 | async-start | bytes 262144 | tf_op jit(solution)/shard_map/all_to_all | solution.py:438
  300.3 12.3 %all-to-all-start.8 = ((bf16[4,64,512]{2,1,0:T(8,128)(2,1)}), bf16[4,64,512]{2,1,0:T(8,128)(2,1)S(1)}, u32[]{:S(2)}, u32[]{:S(2)}) async-start(bf16[4,64,512]{2,1,0:T(8,128)(2,1)} %pad_maximum_fusion), calls=%async_computation.8 | async-start | bytes 524288 | tf_op jit(solution)/shard_map/all_to_all | solution.py:446
